TPU v7x, 32 devices: a whole 2x2x4 slice. The times are simulated.
32 devices in a mesh: client: 16 (over z, y, core), tp: 2 (over x).
Axes of the slice: x: 2, y: 2, z: 4, core: 2. Of those that a mesh axis runs over, the one named last changes fastest.
Arguments:
- tokens: bfloat16 [4096, 2048], P('client'), may hold values from -6 to 6
- targets: bfloat16 [4096, 2048], P('client'), may hold values from -6 to 6
- norm_gain: float32 [2048], replicated, may hold values from 0.25 to 1.75
- up_frozen: bfloat16 [2048, 7168], P('client', 'tp'), may hold values from -0.125 to 0.125
- down_frozen: bfloat16 [7168, 2048], P('tp', 'client'), may hold values from -0.0625 to 0.0625
- up_left: float32 [16, 2048], replicated, may hold values from -1 to 1
- up_right: float32 [16, 7168], P(None, 'tp'), may hold values from -0.4375 to 0.4375
- down_left: float32 [16, 7168], P(None, 'tp'), may hold values from -0.625 to 0.625
- down_right: float32 [16, 2048], replicated, may hold values from -0.0625 to 0.0625
- counts: int32 [16], P('client'), may hold values from 64 to 4096
Outputs:
- round_up_left: float32 [16, 2048], replicated
- round_up_right: float32 [16, 7168], P(None, 'tp')
- round_down_left: float32 [16, 7168], P(None, 'tp')
- round_down_right: float32 [16, 2048], replicated
All inputs are finite; a program needn't handle non-finite values.
Results may differ from a plain program's by a relative error of at most 0.0089.
Values may be sent and summed in bfloat16 or wider, within the bound.
A program may use at most 128 MiB of HBM per device.

v0:
```python
import jax
import jax.numpy as jnp
from jax import lax
from jax.sharding import PartitionSpec as P

STEPS = 3


LEARN_RATE = 0.01
PROX_WEIGHT = 10.0
ADAPTER_SCALING = 0.5
NORM_EPS = 1e-05


def contracted_rows(left, right):
    return lax.dot_general(
        left, right, (((0,), (0,)), ((), ())), preferred_element_type=jnp.float32
    )


def contract_columns(left, right):
    return lax.dot_general(
        left, right, (((1,), (1,)), ((), ())), preferred_element_type=jnp.float32
    )


def update(value, grad, anchor):
    return value - LEARN_RATE * (grad + PROX_WEIGHT * (value - anchor))


def per_device(
    tokens,
    targets,
    norm_gain,
    up_frozen,
    down_frozen,
    up_left,
    up_right,
    down_left,
    down_right,
    counts,
):
    token_count = tokens.shape[0]
    wide = tokens.astype(jnp.float32)
    scale = lax.rsqrt(jnp.mean(wide * wide, axis=1, keepdims=True) + NORM_EPS)
    normalized_input = (wide * scale * norm_gain).astype(jnp.bfloat16)
    whole_up = lax.all_gather(up_frozen, "client", axis=0, tiled=True)
    frozen_hidden_rows = jnp.dot(normalized_input, whole_up, preferred_element_type=jnp.float32)
    whole_down = lax.all_gather(down_frozen, "client", axis=1, tiled=True)
    start = (up_left, up_right, down_left, down_right)
    params = start
    for local_step in range(STEPS):
        up_left_b = params[0].astype(jnp.bfloat16)
        up_right_batch = params[1].astype(jnp.bfloat16)
        down_left_b = params[2].astype(jnp.bfloat16)
        down_right_batch = params[3].astype(jnp.bfloat16)
        up_low_product = contract_columns(normalized_input, up_left_b).astype(jnp.bfloat16)
        hidden_preactivation = frozen_hidden_rows + ADAPTER_SCALING * jnp.dot(
            up_low_product, up_right_batch, preferred_element_type=jnp.float32
        )
        gated_hidden = jax.nn.silu(hidden_preactivation).astype(jnp.bfloat16)
        partial_value = jnp.dot(gated_hidden, whole_down, preferred_element_type=jnp.float32)
        low_part = contract_columns(gated_hidden, down_left_b)
        share_width = partial_value.shape[1] // lax.axis_size("tp")
        offset = lax.axis_index("tp") * share_width
        summed = lax.psum_scatter(partial_value, "tp", scatter_dimension=1, tiled=True)
        down_low_product = lax.psum(low_part, "tp").astype(jnp.bfloat16)
        right_share = lax.dynamic_slice_in_dim(down_right_batch, offset, share_width, 1)
        token_share = lax.dynamic_slice_in_dim(tokens, offset, share_width, 1)
        target_share = lax.dynamic_slice_in_dim(targets, offset, share_width, 1)
        layer_output = token_share.astype(jnp.float32) + summed
        layer_output = layer_output + ADAPTER_SCALING * jnp.dot(
            down_low_product, right_share, preferred_element_type=jnp.float32
        )
        d_share = ((layer_output - target_share.astype(jnp.float32)) / token_count).astype(
            jnp.bfloat16
        )
        output_gradient = lax.all_gather(d_share, "tp", axis=1, tiled=True)
        down_low_gradient = (
            ADAPTER_SCALING * contract_columns(output_gradient, down_right_batch)
        ).astype(jnp.bfloat16)
        d_gated = contract_columns(output_gradient, whole_down) + jnp.dot(
            down_low_gradient, down_left_b, preferred_element_type=jnp.float32
        )
        sigmoid_pre = jax.nn.sigmoid(hidden_preactivation)
        hidden_gradient = (
            d_gated * sigmoid_pre * (1.0 + hidden_preactivation * (1.0 - sigmoid_pre))
        ).astype(jnp.bfloat16)
        low_rank_gradient = lax.psum(
            ADAPTER_SCALING * contract_columns(hidden_gradient, up_right_batch), "tp"
        )
        up_low_gradient = low_rank_gradient.astype(jnp.bfloat16)
        gradient_tree = (
            contracted_rows(up_low_gradient, normalized_input),
            ADAPTER_SCALING * contracted_rows(up_low_product, hidden_gradient),
            contracted_rows(down_low_gradient, gated_hidden),
            ADAPTER_SCALING * contracted_rows(down_low_product, output_gradient),
        )
        params = jax.tree.map(update, params, gradient_tree, start)
    weight = counts.astype(jnp.float32)

    def weighted(anchor, value):
        return weight[0] * (anchor - value)

    deltas = jax.tree.map(weighted, start, params)
    sums = lax.psum((deltas[0], deltas[1], deltas[2], deltas[3], weight), "client")
    factor = LEARN_RATE * sums[4][0]
    return (sums[0] / factor, sums[1] / factor, sums[2] / factor, sums[3] / factor)


def solution(mesh):
    placed = (
        P("client", None),
        P("client", None),
        P(),
        P("client", "tp"),
        P("tp", "client"),
        P(),
        P(None, "tp"),
        P(None, "tp"),
        P(),
        P("client"),
    )
    return jax.shard_map(
        per_device,
        mesh=mesh,
        in_specs=placed,
        out_specs=(P(), P(None, "tp"), P(None, "tp"), P()),
        check_vma=False,
    )
```

profile of v0, /device:TPU:0, one launch (start us, length us, event | category | flops | bytes accessed | tf_op | source)
XLA Modules:
  0.0 624.4 jit_solution(11934358948694620464)
XLA Ops:
  8.7 1.5 fusion.50
  10.2 1.7 convolution_convert_fusion.2
  11.9 114.4 %all-gather.6.cloned.1.call-done = bf16[2048,3584]{1,0:T(8,128)(2,1)} async-done(((bf16[128,3584]{1,0:T(8,128)(2,1)}), bf16[2048,3584]{1,0:T(8,128)(2,1)}) %all-gather.6.cloned.1.call-update) | async-done | bytes 14680080 | tf_op jit(solution)/shard_map/all_gather | solution.py:47
  126.4 7.4 %fusion.104 = f32[256,3584]{1,0:T(8,128)S(1)} fusion(bf16[2048,3584]{1,0:T(8,128)(2,1)} %all-gather.6.cloned.1.call-done, bf16[256,2048]{1,0:T(8,128)(2,1)S(1)} %copy-done.3, f32[2048]{0:T(1024)S(1)} %copy-done.30, f32[256]{0:T(256)S(1)} %add_rsqrt_fusion), kind=kOutput, calls=%fused_computation.147 | convolution fusion | flops 3760193536 | bytes 19407872 | tf_op jit(solution)/shard_map/dot_general | solution.py:48
  133.8 1.8 copy-done.37
  135.6 3.1 multiply_convert_fusion.2
  138.7 104.7 %all-gather.8.cloned.1.call-done = bf16[3584,2048]{1,0:T(8,128)(2,1)} async-done(((bf16[3584,128]{1,0:T(8,128)(2,1)}), bf16[3584,2048]{1,0:T(8,128)(2,1)}) %all-gather.8.cloned.1.call-update) | async-done | bytes 14680080 | tf_op jit(solution)/shard_map/all_gather | solution.py:49
  243.4 8.8 %fusion.108 = f32[256,2048]{1,0:T(8,128)} fusion(bf16[256,3584]{1,0:T(8,128)(2,1)S(1)} %get-tuple-element.8, bf16[3584,2048]{1,0:T(8,128)(2,1)} %all-gather.8.cloned.1.call-done), kind=kOutput, calls=%fused_computation.150 | convolution fusion | flops 3758096384 | bytes 18612224 | tf_op jit(solution)/shard_map/dot_general | solution.py:62
  252.3 1.2 fusion.79
  253.5 9.4 %psum.77 = bf16[256,16]{0,1:T(8,128)(2,1)S(1)} all-reduce(f32[256,16]{0,1:T(8,128)} %fusion.79), channel_id=1, replica_groups=mesh['client'=16,'tp'=2] {'tp'}, use_global_device_ids=true, to_apply=%region_2.3 | all-reduce | flops 4096 | bytes 24576 | tf_op jit(solution)/shard_map/psum | solution.py:67
  262.9 19.8 %reduce-scatter.4.cloned.1.call-done = f32[256,1024]{1,0:T(8,128)} async-done(((f32[256,2048]{1,0:T(8,128)}), f32[256,1024]{1,0:T(8,128)}) %reduce-scatter.4.cloned.1.call-update) | async-done | bytes 1048592 | tf_op jit(solution)/shard_map/reduce_scatter | solution.py:66
  282.7 2.5 fusion.59
  285.3 21.2 %all-gather.10.cloned.1.call-done = bf16[256,2048]{1,0:T(8,128)(2,1)} async-done(((bf16[256,1024]{1,0:T(8,128)(2,1)}), bf16[256,2048]{1,0:T(8,128)(2,1)}) %all-gather.10.cloned.1.call-update) | async-done | bytes 1048592 | tf_op jit(solution)/shard_map/all_gather | solution.py:78
  306.5 9.5 %fusion.109 = f32[256,3584]{1,0:T(8,128)S(1)} fusion(bf16[256,2048]{1,0:T(8,128)(2,1)} %all-gather.10.cloned.1.call-done, bf16[3584,2048]{1,0:T(8,128)(2,1)} %all-gather.8.cloned.1.call-done), kind=kOutput, calls=%fused_computation.151 | convolution fusion | flops 3758096384 | bytes 19398656 | tf_op jit(solution)/shard_map/dot_general | solution.py:22
  316.4 3.7 fusion.9
  321.7 7.0 %psum.78 = bf16[256,16]{0,1:T(8,128)(2,1)S(1)} all-reduce(f32[256,16]{0,1:T(8,128)S(1)} %convolution_multiply_fusion.16), channel_id=1, replica_groups=mesh['client'=16,'tp'=2] {'tp'}, use_global_device_ids=true, to_apply=%region_3.4 | all-reduce | flops 4096 | bytes 24576 | tf_op jit(solution)/shard_map/psum | solution.py:89
  331.0 3.1 multiply_convert_fusion.1
  334.1 8.7 %fusion.110 = f32[256,2048]{1,0:T(8,128)} fusion(bf16[256,3584]{1,0:T(8,128)(2,1)S(1)} %get-tuple-element.10, bf16[3584,2048]{1,0:T(8,128)(2,1)} %all-gather.8.cloned.1.call-done), kind=kOutput, calls=%fused_computation.152 | convolution fusion | flops 3758096384 | bytes 18612224 | tf_op jit(solution)/shard_map/dot_general | solution.py:62
  342.8 1.9 fusion.27
  345.9 8.8 %psum.79 = bf16[256,16]{0,1:T(8,128)(2,1)S(1)} all-reduce(f32[256,16]{0,1:T(8,128)S(1)} %fusion.74), channel_id=1, replica_groups=mesh['client'=16,'tp'=2] {'tp'}, use_global_device_ids=true, to_apply=%region_5.6 | all-reduce | flops 4096 | bytes 24576 | tf_op jit(solution)/shard_map/psum | solution.py:67
  354.7 2.1 fusion.106
  356.9 19.2 %reduce-scatter.6.cloned.1.call-done = f32[256,1024]{1,0:T(8,128)} async-done(((f32[256,2048]{1,0:T(8,128)}), f32[256,1024]{1,0:T(8,128)}) %reduce-scatter.6.cloned.1.call-update) | async-done | bytes 1048592 | tf_op jit(solution)/shard_map/reduce_scatter | solution.py:66
  376.1 2.6 fusion.60
  378.8 21.5 %all-gather.12.cloned.1.call-done = bf16[256,2048]{1,0:T(8,128)(2,1)} async-done(((bf16[256,1024]{1,0:T(8,128)(2,1)}), bf16[256,2048]{1,0:T(8,128)(2,1)}) %all-gather.12.cloned.1.call-update) | async-done | bytes 1048592 | tf_op jit(solution)/shard_map/all_gather | solution.py:78
  400.2 1.6 fusion.63
  401.8 7.6 %fusion.111 = f32[256,3584]{1,0:T(8,128)S(1)} fusion(bf16[256,2048]{1,0:T(8,128)(2,1)} %all-gather.12.cloned.1.call-done, bf16[3584,2048]{1,0:T(8,128)(2,1)} %all-gather.8.cloned.1.call-done), kind=kOutput, calls=%fused_computation.153 | convolution fusion | flops 3758096384 | bytes 19398656 | tf_op jit(solution)/shard_map/dot_general | solution.py:22
  409.5 3.7 fusion.10
  414.9 7.0 %psum.80 = bf16[256,16]{0,1:T(8,128)(2,1)S(1)} all-reduce(f32[256,16]{0,1:T(8,128)S(1)} %convolution_multiply_fusion.14), channel_id=1, replica_groups=mesh['client'=16,'tp'=2] {'tp'}, use_global_device_ids=true, to_apply=%region_6.7 | all-reduce | flops 4096 | bytes 24576 | tf_op jit(solution)/shard_map/psum | solution.py:89
  422.0 1.5 fusion.44
  424.6 3.0 multiply_convert_fusion
  427.7 1.3 copy-done.1
  428.9 8.7 %fusion.112 = f32[256,2048]{1,0:T(8,128)} fusion(bf16[256,3584]{1,0:T(8,128)(2,1)S(1)} %get-tuple-element.14, bf16[3584,2048]{1,0:T(8,128)(2,1)} %all-gather.8.cloned.1.call-done), kind=kOutput, calls=%fused_computation.154 | convolution fusion | flops 3758096384 | bytes 18612224 | tf_op jit(solution)/shard_map/dot_general | solution.py:62
  437.7 1.3 fusion.22
  439.7 2.2 fusion.69
  441.9 8.9 %psum.81 = bf16[256,16]{0,1:T(8,128)(2,1)S(1)} all-reduce(f32[256,16]{0,1:T(8,128)S(1)} %fusion.69), channel_id=1, replica_groups=mesh['client'=16,'tp'=2] {'tp'}, use_global_device_ids=true, to_apply=%region_8.9 | all-reduce | flops 4096 | bytes 24576 | tf_op jit(solution)/shard_map/psum | solution.py:67
  450.8 2.1 fusion.107
  452.9 18.1 %reduce-scatter.8.cloned.1.call-done = f32[256,1024]{1,0:T(8,128)} async-done(((f32[256,2048]{1,0:T(8,128)}), f32[256,1024]{1,0:T(8,128)}) %reduce-scatter.8.cloned.1.call-update) | async-done | bytes 1048592 | tf_op jit(solution)/shard_map/reduce_scatter | solution.py:66
  471.0 2.6 fusion.61
  474.3 20.8 %all-gather.14.cloned.1.call-done = bf16[256,2048]{1,0:T(8,128)(2,1)} async-done(((bf16[256,1024]{1,0:T(8,128)(2,1)}), bf16[256,2048]{1,0:T(8,128)(2,1)}) %all-gather.14.cloned.1.call-update) | async-done | bytes 1048592 | tf_op jit(solution)/shard_map/all_gather | solution.py:78
  495.1 1.6 fusion.64
  496.7 2.0 fusion.15
  498.7 7.6 %fusion.113 = f32[256,3584]{1,0:T(8,128)S(1)} fusion(bf16[256,2048]{1,0:T(8,128)(2,1)} %all-gather.14.cloned.1.call-done, bf16[3584,2048]{1,0:T(8,128)(2,1)} %all-gather.8.cloned.1.call-done), kind=kOutput, calls=%fused_computation.155 | convolution fusion | flops 3758096384 | bytes 19398656 | tf_op jit(solution)/shard_map/dot_general | solution.py:22
  506.4 3.7 fusion.11
  511.8 7.0 %psum.82 = bf16[256,16]{0,1:T(8,128)(2,1)S(1)} all-reduce(f32[256,16]{0,1:T(8,128)S(1)} %convolution_multiply_fusion.12), channel_id=1, replica_groups=mesh['client'=16,'tp'=2] {'tp'}, use_global_device_ids=true, to_apply=%region_9.10 | all-reduce | flops 4096 | bytes 24576 | tf_op jit(solution)/shard_map/psum | solution.py:89
  520.9 32.8 %psum.84 = f32[1]{0:T(128)} all-reduce(f32[1]{0:T(128)} %convert_element_type.118), channel_id=1, replica_groups=mesh['client'=16,'tp'=2] {'client'}, use_global_device_ids=true, to_apply=%region_11.12 | all-reduce | flops 1 | bytes 8 | tf_op jit(solution)/shard_map/psum | solution.py:106
  554.4 60.0 %all-reduce.3.cloned.1.call-done = (f32[16,2048]{1,0:T(8,128)}, f32[16,3584]{1,0:T(8,128)}, f32[16,3584]{1,0:T(8,128)}, f32[16,2048]{1,0:T(8,128)}) async-done(((f32[16,2048]{1,0:T(8,128)}, f32[16,3584]{1,0:T(8,128)}, f32[16,3584]{1,0:T(8,128)}, f32[16,2048]{1,0:T(8,128)}), (f32[16,2048]{1,0:T(8,128)}, f32[16,3584]{1,0:T(8,128)}, f32[16,3584]{1,0:T(8,128)}, ...) | async-done | bytes 720912 | tf_op jit(solution)/shard_map/psum | solution.py:106
  614.3 1.8 broadcast_divide_fusion
  616.2 1.7 broadcast_divide_fusion.2
  (111 shorter events, 14.5 us)
Async XLA Ops:
  7.2 119.2 %copy-start.3 = (bf16[256,2048]{1,0:T(8,128)(2,1)S(1)}, bf16[256,2048]{1,0:T(8,128)(2,1)}, u32[]{:S(2)}) copy-start(bf16[256,2048]{1,0:T(8,128)(2,1)} %param.10) | copy-start | bytes 3145732
  7.2 119.2 %copy-start.30 = (f32[2048]{0:T(1024)S(1)}, f32[2048]{0:T(1024)}, u32[]{:S(2)}) copy-start(f32[2048]{0:T(1024)} %param.12) | copy-start | bytes 24580
  7.2 119.2 %all-gather.6.cloned.1.call-start = ((), (), s32[]{:S(2)}) async-start(), calls=%async_computation.3 | async-start | bytes 15597568 | tf_op jit(solution)/shard_map/all_gather | solution.py:47
  7.9 235.5 %all-gather.8.cloned.1.call-start = ((), (), s32[]{:S(2)}) async-start(), calls=%async_computation.4 | async-start | bytes 15597568 | tf_op jit(solution)/shard_map/all_gather | solution.py:49
  8.7 274.0 %reduce-scatter.4.cloned.1.call-start = ((), (), s32[]{:S(2)}) async-start(), calls=%async_computation.5 | async-start | bytes 3145728 | tf_op jit(solution)/shard_map/reduce_scatter | solution.py:66
  10.2 123.5 %copy-start.24 = (f32[256]{0:T(256)}, f32[256]{0:T(256)S(1)}, u32[]{:S(2)}) copy-start(f32[256]{0:T(256)S(1)} %add_rsqrt_fusion) | copy-start | bytes 3076
  11.9 121.8 %copy-start.18 = (bf16[256,16]{0,1:T(8,128)(2,1)}, bf16[256,16]{0,1:T(8,128)(2,1)S(1)}, u32[]{:S(2)}) copy-start(bf16[256,16]{0,1:T(8,128)(2,1)S(1)} %convolution_convert_fusion.2) | copy-start | bytes 24580
  11.9 123.7 %copy-start.7 = (f32[16,3584]{1,0:T(8,128)S(1)}, f32[16,3584]{1,0:T(8,128)}, u32[]{:S(2)}) copy-start(f32[16,3584]{1,0:T(8,128)} %param.16) | copy-start | bytes 688132
  133.8 1.8 copy-start.37
  138.7 113.6 %copy-start = (bf16[256,3584]{1,0:T(8,128)(2,1)}, bf16[256,3584]{1,0:T(8,128)(2,1)S(1)}, u32[]{:S(2)}) copy-start(bf16[256,3584]{1,0:T(8,128)(2,1)S(1)} %get-tuple-element.8) | copy-start | bytes 5505028
  243.4 8.8 %copy-start.8 = (f32[16,2048]{1,0:T(8,128)S(1)}, f32[16,2048]{1,0:T(8,128)}, u32[]{:S(2)}) copy-start(f32[16,2048]{1,0:T(8,128)} %param.18) | copy-start | bytes 393220
  243.4 8.9 %copy-start.6 = (f32[16,3584]{1,0:T(8,128)S(1)}, f32[16,3584]{1,0:T(8,128)}, u32[]{:S(2)}) copy-start(f32[16,3584]{1,0:T(8,128)} %param.17) | copy-start | bytes 688132
  252.2 54.3 %all-gather.10.cloned.1.call-start = ((), (), s32[]{:S(2)}) async-start(), calls=%async_computation.6 | async-start | bytes 1572864 | tf_op jit(solution)/shard_map/all_gather | solution.py:78
  285.2 90.9 %reduce-scatter.6.cloned.1.call-start = ((), (), s32[]{:S(2)}) async-start(), calls=%async_computation.7 | async-start | bytes 3145728 | tf_op jit(solution)/shard_map/reduce_scatter | solution.py:66
  306.5 9.5 %copy-start.4 = (bf16[256,2048]{1,0:T(8,128)(2,1)S(1)}, bf16[256,2048]{1,0:T(8,128)(2,1)}, u32[]{:S(2)}) copy-start(bf16[256,2048]{1,0:T(8,128)(2,1)} %all-gather.10.cloned.1.call-done) | copy-start | bytes 3145732
  316.4 3.7 copy-start.19
  320.1 8.7 %copy-start.25 = (f32[256]{0:T(256)S(1)}, f32[256]{0:T(256)}, u32[]{:S(2)}) copy-start(f32[256]{0:T(256)} %copy-done.24) | copy-start | bytes 3076
  320.1 8.7 %copy-start.28 = (f32[16,2048]{1,0:T(8,128)S(1)}, f32[16,2048]{1,0:T(8,128)}, u32[]{:S(2)}) copy-start(f32[16,2048]{1,0:T(8,128)} %param.15) | copy-start | bytes 393220
  320.1 8.7 %copy-start.31 = (f32[2048]{0:T(1024)S(1)}, f32[2048]{0:T(1024)}, u32[]{:S(2)}) copy-start(f32[2048]{0:T(1024)} %param.12) | copy-start | bytes 24580
  328.8 1.6 copy-start.11
  328.8 2.2 copy-start.38
  329.2 0.7 copy-start.36
  331.0 3.1 copy-start.22
  342.8 57.5 %all-gather.12.cloned.1.call-start = ((), (), s32[]{:S(2)}) async-start(), calls=%async_computation.8 | async-start | bytes 1572864 | tf_op jit(solution)/shard_map/all_gather | solution.py:78
  344.7 0.7 copy-start.9
  378.7 92.3 %reduce-scatter.8.cloned.1.call-start = ((), (), s32[]{:S(2)}) async-start(), calls=%async_computation.9 | async-start | bytes 3145728 | tf_op jit(solution)/shard_map/reduce_scatter | solution.py:66
  401.8 7.7 %copy-start.10 = (f32[16,3584]{1,0:T(8,128)S(1)}, f32[16,3584]{1,0:T(8,128)}, u32[]{:S(2)}) copy-start(f32[16,3584]{1,0:T(8,128)} %copy-done.9) | copy-start | bytes 688132
  409.5 3.7 copy-start.12
  409.5 3.7 copy-start.23
  413.3 8.7 %copy-start.26 = (f32[256]{0:T(256)S(1)}, f32[256]{0:T(256)}, u32[]{:S(2)}) copy-start(f32[256]{0:T(256)} %copy-done.24) | copy-start | bytes 3076
  413.3 8.7 %copy-start.32 = (f32[2048]{0:T(1024)S(1)}, f32[2048]{0:T(1024)}, u32[]{:S(2)}) copy-start(f32[2048]{0:T(1024)} %param.12) | copy-start | bytes 24580
  421.9 2.7 copy-start.13
  421.9 2.7 copy-start.39
  424.6 3.1 copy-start.20
  427.7 1.3 copy-start.1
  437.7 57.4 %all-gather.14.cloned.1.call-start = ((), (), s32[]{:S(2)}) async-start(), calls=%async_computation.10 | async-start | bytes 1572864 | tf_op jit(solution)/shard_map/all_gather | solution.py:78
  439.0 0.7 copy-start.15
  439.7 57.0 %copy-start.2 = (bf16[256,3584]{1,0:T(8,128)(2,1)S(1)}, bf16[256,3584]{1,0:T(8,128)(2,1)}, u32[]{:S(2)}) copy-start(bf16[256,3584]{1,0:T(8,128)(2,1)} %copy-done.1) | copy-start | bytes 5505028
  473.6 140.7 %all-reduce.3.cloned.1.call-start = ((), (), s32[]{:S(2)}) async-start(), calls=%async_computation.11 | async-start | bytes 1441792 | tf_op jit(solution)/shard_map/psum | solution.py:106
  498.7 7.6 %copy-start.16 = (f32[16,3584]{1,0:T(8,128)S(1)}, f32[16,3584]{1,0:T(8,128)}, u32[]{:S(2)}) copy-start(f32[16,3584]{1,0:T(8,128)} %copy-done.15) | copy-start | bytes 688132
  506.4 3.7 copy-start.14
  506.4 3.7 copy-start.21
  510.1 8.7 %copy-start.27 = (f32[256]{0:T(256)S(1)}, f32[256]{0:T(256)}, u32[]{:S(2)}) copy-start(f32[256]{0:T(256)} %copy-done.24) | copy-start | bytes 3076
  510.1 8.7 %copy-start.29 = (f32[16,2048]{1,0:T(8,128)S(1)}, f32[16,2048]{1,0:T(8,128)}, u32[]{:S(2)}) copy-start(f32[16,2048]{1,0:T(8,128)} %param.15) | copy-start | bytes 393220
  510.1 8.7 %copy-start.33 = (f32[2048]{0:T(1024)S(1)}, f32[2048]{0:T(1024)}, u32[]{:S(2)}) copy-start(f32[2048]{0:T(1024)} %param.12) | copy-start | bytes 24580
  510.1 8.7 %copy-start.35 = (f32[16,2048]{1,0:T(8,128)S(1)}, f32[16,2048]{1,0:T(8,128)}, u32[]{:S(2)}) copy-start(f32[16,2048]{1,0:T(8,128)} %copy-done.34) | copy-start | bytes 393220
  510.2 9.8 %copy-start.5 = (bf16[256,2048]{1,0:T(8,128)(2,1)S(1)}, bf16[256,2048]{1,0:T(8,128)(2,1)}, u32[]{:S(2)}) copy-start(bf16[256,2048]{1,0:T(8,128)(2,1)} %all-gather.14.cloned.1.call-done) | copy-start | bytes 3145732
  510.2 9.8 %copy-start.17 = (f32[16,2048]{1,0:T(8,128)S(1)}, f32[16,2048]{1,0:T(8,128)}, u32[]{:S(2)}) copy-start(f32[16,2048]{1,0:T(8,128)} %get-tuple-element.17) | copy-start | bytes 393220
  (1 other events, 0.7 us)
Sparse Core Ops, SparseCore 0:
  10.3 116.0 all-gather.5
  128.5 114.8 all-gather.7
  252.3 30.3 reduce-scatter.3
  285.4 21.0 all-gather.9
  342.9 33.1 reduce-scatter.5
  378.8 21.3 all-gather.11
  437.8 33.1 reduce-scatter.7
  473.7 21.3 all-gather.13
  521.0 93.3 all-reduce.2
where the time goes:
time: 625 us; the launch traced here: 624 us
  waiting for transfers between devices  401 us (64%)
  matrix products  115 us (18%)
  blocking collectives  81 us (13%)
  between operations  15.6 us (2%)
  local copies, waits for them, and re-layouts  6.61 us (1%)
    all_gather x1, waiting for transfers between devices, per_device(): whole_up = lax.all_gather(up_frozen, 'client', axis=0, tiled=True)  114 us
    all_gather x1, waiting for transfers between devices, per_device(): whole_down = lax.all_gather(down_frozen, 'client', axis=1, tiled=True)  105 us
    all_gather x3, waiting for transfers between devices, per_device(): output_gradient = lax.all_gather(d_share, 'tp', axis=1, tiled=True)  63.5 us
    psum x1, waiting for transfers between devices, per_device(): lax.psum((deltas[0], deltas[1], deltas[2], deltas[3], weight), 'client')  60 us
    reduce_scatter x3, waiting for transfers between devices, per_device(): lax.psum_scatter(partial_value, 'tp', scatter_dimension=1, tiled=True)  57.1 us
    dot_general x15, matrix products, contract_columns(): lax.dot_general(left, right, (((1,), (1,)), ((), ())), preferred_element_...  36.5 us
    psum x1, blocking collectives, per_device(): lax.psum((deltas[0], deltas[1], deltas[2], deltas[3], weight), 'client')  32.8 us
    psum x3, blocking collectives, per_device(): down_low_product = lax.psum(low_part, 'tp').astype(jnp.bfloat16)  27.1 us
  transfers between devices with their start and end apart: 9, of which 9 were waited for; matrix products, arithmetic and copies ran while one was open for 4% of the time, Pallas kernels for 0%

commit v1 on v0

v1 whole, which is shorter than its diff:
```python
import functools

import jax
import jax.numpy as jnp
from jax import lax
from jax.experimental import pallas as pl
from jax.experimental.pallas import tpu as pltpu
from jax.sharding import PartitionSpec as P

STEPS = 3
LEARN_RATE = 0.01
PROX_WEIGHT = 10.0
ADAPTER_SCALING = 0.5
NORM_EPS = 1e-05

F32 = jnp.float32
BF16 = jnp.bfloat16


def mm(a, b):
    return lax.dot_general(a, b, (((1,), (0,)), ((), ())), preferred_element_type=F32)


def mmt(a, b):
    return lax.dot_general(a, b, (((1,), (1,)), ((), ())), preferred_element_type=F32)


def update(value, grad, anchor):
    return value - LEARN_RATE * (grad + PROX_WEIGHT * (value - anchor))


def kernel(n, subs, bpd, tile, up, dnt, nx, diff, ul0, ur0, dl0, dr0, cnt,
           oul, our, odl, odr,
           w0, w1, base, dact, gate, act, ptx, prx, dout,
           ul, ur, dl, dr, ulb, drb, urb, dlb,
           lut, ldt, dldt, ldm, xtx, xrx, cntb,
           sbuf, abuf, bbuf, cbuf, rbuf,
           own_s, ring_s, ring_r, sib_s, sib_r, p_s, p_r, x_s, x_r, c_s, c_r,
           ab_s, ab_r, b_s, b_r, g_s, g_r):
    R = n // 2
    half_ring = R // 2
    me = lax.axis_index("client")
    tp = lax.axis_index("tp")
    chip = me // 2
    core = me % 2
    sib = chip * 2 + (1 - core)
    ws = (w0, w1)
    cr, ffl = w0.shape[1], w0.shape[2]
    rows = cr // 2
    piece = rows // (2 * subs)
    tok = nx.shape[1]
    n_tiles = ffl // tile

    low = chip % 2
    pos = jnp.where(low == 0, chip // 2, R - 1 - chip // 2)

    def chip_at(p):
        p = (p + 2 * R) % R
        return jnp.where(p < half_ring, 2 * p, 2 * (R - 1 - p) + 1)

    def copy(src, dst, ss, rs, client, t):
        return pltpu.make_async_remote_copy(
            src_ref=src, dst_ref=dst, send_sem=ss, recv_sem=rs,
            device_id={"client": client, "tp": t},
            device_id_type=pl.DeviceIdType.MESH)

    nbr = (chip_at(pos + 1) * 2 + core, chip_at(pos - 1) * 2 + core)

    def place(m, d, s, u, c):
        origin = chip_at(pos - s) if d == 0 else chip_at(pos + s)
        start = pl.multiple_of(c * rows + (d * subs + u) * piece, piece)
        return ws[m].at[origin, pl.ds(start, piece)]

    def ring_copy(m, d, s, u):
        ref = place(m, d, s, u, core)
        nxt = jnp.minimum(s + 1, R - 1)
        return copy(ref, ref, ring_s.at[m, d, s, u], ring_r.at[m, d, nxt, u], nbr[d], tp)

    def ring_arrived(m, d, s, u):
        ref = place(m, d, s, u, core)
        copy(ref, ref, ring_s.at[m, d, s, u], ring_r.at[m, d, s, u], nbr[d], tp).wait_recv()

    def sib_copy(m, d, s, u, c):
        ref = place(m, d, s, u, c)
        return copy(ref, ref, sib_s.at[m, d, s, u], sib_r.at[m, d, s, u], sib, tp)

    def send_own(m):
        for u in range(subs):
            for d in range(2):
                ring_copy(m, d, 0, u).start()
        for u in range(subs):
            for d in range(2):
                sib_copy(m, d, 0, u, core).start()

    def advance(m, s, forward):
        for u in range(subs):
            for d in range(2):
                ring_arrived(m, d, s, u)
                if forward:
                    ring_copy(m, d, s, u).start()
                sib_copy(m, d, s, u, core).start()

    def sib_arrived(m, dist):
        for u in range(subs):
            sib_copy(m, 0, dist, u, 1 - core).wait_recv()
            sib_copy(m, 1, (R - dist) % R, u, 1 - core).wait_recv()

    def tiles(fn, init=0):
        return lax.fori_loop(
            0, n_tiles, lambda i, c: fn(pl.ds(pl.multiple_of(i * tile, tile), tile), c), init)

    own_rows = pl.ds(pl.multiple_of(core * rows, rows), rows)
    own0 = pltpu.make_async_copy(up, w0.at[chip, own_rows], own_s.at[0])
    own1 = pltpu.make_async_copy(dnt, w1.at[chip, own_rows], own_s.at[1])
    own0.start()
    own1.start()
    own0.wait()
    send_own(0)

    cntb[me] = cnt[...]

    def cnt_copy(k):
        return copy(cntb.at[me], cntb.at[me], c_s.at[k], c_r.at[me], k, tp)

    @pl.loop(1, n)
    def _(i):
        cnt_copy((me + i) % n).start()

    base[...] = jnp.zeros_like(base)
    ul[...] = ul0[...]
    ur[...] = ur0[...]
    dl[...] = dl0[...]
    dr[...] = dr0[...]

    def add_base(dist):
        sib_arrived(0, dist)
        j = chip_at(pos - dist)

        def body(cols, c):
            base[:, cols] += mm(nx[j], w0[j, :, cols])
            return c
        tiles(body)

    def forward_piece(j):
        ptx[j] = mmt(act[...], w1[j]).astype(BF16)
        copy(ptx.at[j], prx.at[j], p_s.at[j], p_r.at[j], me, 1 - tp).start()

    def backward_piece(j):
        copy(ptx.at[j], prx.at[j], p_s.at[j], p_r.at[j], me, 1 - tp).wait_recv()
        total = ptx[j].astype(F32) + prx[j].astype(F32)
        out = diff[j] + total + ADAPTER_SCALING * mm(ldm[...], drb[j])
        grad = (out / tok).astype(BF16)
        dout[j] = grad
        dldt[...] += mmt(drb[j], grad)

        def body(cols, c):
            dact[:, cols] += mm(grad, w1[j, :, cols])
            return c
        tiles(body)

    def x_copy(k):
        return copy(xtx.at[k], xrx.at[k], x_s.at[k], x_r.at[k], me, 1 - tp)

    def begin_step():
        for j in range(R):
            ulb[j] = ul[:, j * cr:(j + 1) * cr].astype(BF16)
            drb[j] = dr[:, j * cr:(j + 1) * cr].astype(BF16)
        urb[...] = ur[...].astype(BF16)
        dlb[...] = dl[...].astype(BF16)
        low_t = lax.fori_loop(
            0, R, lambda j, c: c + mmt(ulb[j], nx[j]), jnp.zeros((ul.shape[0], tok), F32))
        lut[...] = low_t.astype(BF16)
        lu = low_t.T.astype(BF16)

        def body(cols, c):
            pre = base[:, cols] + ADAPTER_SCALING * mm(lu, urb[:, cols])
            sig = jax.nn.sigmoid(pre)
            a = (pre * sig).astype(BF16)
            act[:, cols] = a
            gate[:, cols] = sig * (1.0 + pre * (1.0 - sig))
            dact[:, cols] = jnp.zeros((tok, tile), F32)
            return c + mmt(dlb[:, cols], a)
        xtx[0] = tiles(body, jnp.zeros((ul.shape[0], tok), F32))
        x_copy(0).start()
        dldt[...] = jnp.zeros_like(dldt)

    def take_low():
        x_copy(0).wait_recv()
        total = xtx[0] + xrx[0]
        ldt[...] = total.astype(BF16)
        ldm[...] = total.T.astype(BF16)

    def end_step():
        dld = ADAPTER_SCALING * dldt[...]
        dld_t = dld.astype(BF16)
        dld_m = dld.T.astype(BF16)

        def body(cols, c):
            h = ((dact[:, cols] + mm(dld_m, dlb[:, cols])) * gate[:, cols]).astype(BF16)
            ur[:, cols] = update(ur[:, cols], ADAPTER_SCALING * mm(lut[...], h), ur0[:, cols])
            dl[:, cols] = update(dl[:, cols], mm(dld_t, act[:, cols]), dl0[:, cols])
            return c + mmt(urb[:, cols], h)
        xtx[1] = ADAPTER_SCALING * tiles(body, jnp.zeros((ul.shape[0], tok), F32))
        x_copy(1).start()
        for j in range(R):
            cols = slice(j * cr, (j + 1) * cr)
            dr[:, cols] = update(dr[:, cols], ADAPTER_SCALING * mm(ldt[...], dout[j]), dr0[:, cols])
        x_copy(1).wait_recv()
        dlu_t = (xtx[1] + xrx[1]).astype(BF16)
        for j in range(R):
            cols = slice(j * cr, (j + 1) * cr)
            ul[:, cols] = update(ul[:, cols], mm(dlu_t, nx[j]), ul0[:, cols])
        x_copy(0).wait_send()
        x_copy(1).wait_send()

        @pl.loop(0, R)
        def _(j):
            copy(ptx.at[j], prx.at[j], p_s.at[j], p_r.at[j], me, 1 - tp).wait_send()

    add_base(0)

    @pl.loop(1, half_ring)
    def _(s):
        advance(0, s, True)
    advance(0, half_ring, half_ring < R - 1)
    add_base(half_ring)

    @pl.loop(half_ring + 1, R - 1)
    def _(s):
        advance(0, s, True)
        add_base(s)
        add_base(R - s)
    own1.wait()
    send_own(1)
    advance(0, R - 1, False)
    add_base(R - 1)
    add_base(1)
    begin_step()

    def down_at(dist):
        return chip_at(pos - dist)

    sib_arrived(1, 0)
    forward_piece(chip)

    advance(1, 1, True)
    take_low()
    backward_piece(chip)

    @pl.loop(2, half_ring)
    def _(s):
        advance(1, s, True)
    advance(1, half_ring, half_ring < R - 1)
    sib_arrived(1, half_ring)
    forward_piece(down_at(half_ring))

    @pl.loop(half_ring + 1, R - 1)
    def _(s):
        advance(1, s, True)
        sib_arrived(1, s)
        forward_piece(down_at(s))
        sib_arrived(1, R - s)
        forward_piece(down_at(R - s))

        @pl.when(s == half_ring + 1)
        def _():
            backward_piece(down_at(half_ring))

        @pl.when(s > half_ring + 1)
        def _():
            backward_piece(down_at(s - 1))
            backward_piece(down_at(R - s + 1))
    advance(1, R - 1, False)
    sib_arrived(1, R - 1)
    forward_piece(down_at(R - 1))
    sib_arrived(1, 1)
    forward_piece(down_at(1))
    backward_piece(down_at(R - 2))
    backward_piece(down_at(2))
    backward_piece(down_at(R - 1))
    backward_piece(down_at(1))
    end_step()

    @pl.loop(1, STEPS)
    def _(t):
        begin_step()

        @pl.loop(0, R)
        def _(j):
            forward_piece(j)
        take_low()

        @pl.loop(0, R)
        def _(j):
            backward_piece(j)
        end_step()

    lanes = 128
    weight = cnt[0:1, 0:1]
    blocks = []
    for value, anchor, result in ((ul, ul0, oul), (ur, ur0, our), (dl, dl0, odl), (dr, dr0, odr)):
        for b in range(value.shape[1] // lanes):
            blocks.append((value, anchor, result, slice(b * lanes, (b + 1) * lanes)))
    for b in range(n * bpd):
        owner, i = divmod(b, bpd)
        c, k = divmod(owner, R)
        if b < len(blocks):
            value, anchor, _, cols = blocks[b]
            sbuf[c, k, i] = (weight * (anchor[:, cols] - value[:, cols])).astype(BF16)
        else:
            sbuf[c, k, i] = jnp.zeros(sbuf.shape[3:], BF16)
    pair = copy(sbuf.at[1 - core], abuf, ab_s.at[0], ab_r.at[0], sib, tp)
    pair.start()

    @pl.loop(1, n)
    def _(i):
        k = (me + i) % n
        copy(cntb.at[k], cntb.at[k], c_s.at[k], c_r.at[k], k, tp).wait_recv()
    total = lax.fori_loop(0, n, lambda k, c: c + cntb[k], jnp.zeros(cnt.shape, F32))
    factor = LEARN_RATE * total[0:1, 0:1]
    pair.wait_recv()

    @pl.loop(0, R)
    def _(k):
        for i in range(bpd):
            bbuf[k, i] = (sbuf[core, k, i].astype(F32) + abuf[k, i].astype(F32)).astype(BF16)

    def chip_copy(k):
        return copy(bbuf.at[k], cbuf.at[chip], b_s.at[k], b_r.at[chip], k * 2 + core, tp)

    @pl.loop(1, R)
    def _(i):
        chip_copy((chip + i) % R).start()
    cbuf[chip] = bbuf[chip]

    @pl.loop(1, R)
    def _(i):
        k = (chip + i) % R
        copy(bbuf.at[k], cbuf.at[k], b_s.at[k], b_r.at[k], k * 2 + core, tp).wait_recv()
    for i in range(bpd):
        s = lax.fori_loop(
            0, R, lambda k, c: c + cbuf[k, i].astype(F32), jnp.zeros(cbuf.shape[2:], F32))
        rbuf[core, chip, i] = (s / factor).astype(BF16)

    def back_copy(k):
        ref = rbuf.at[core, chip]
        return copy(ref, ref, g_s.at[k], g_r.at[chip], k * 2 + core, tp)

    @pl.loop(1, R)
    def _(i):
        back_copy((chip + i) % R).start()

    @pl.loop(1, R)
    def _(i):
        k = (chip + i) % R
        ref = rbuf.at[core, k]
        copy(ref, ref, g_s.at[k], g_r.at[k], k * 2 + core, tp).wait_recv()
    pair2 = copy(rbuf.at[core], rbuf.at[core], ab_s.at[1], ab_r.at[1], sib, tp)
    pair2.start()
    copy(rbuf.at[1 - core], rbuf.at[1 - core], ab_s.at[1], ab_r.at[1], sib, tp).wait_recv()
    for b in range(len(blocks)):
        owner, i = divmod(b, bpd)
        c, k = divmod(owner, R)
        _, _, result, cols = blocks[b]
        result[:, cols] = rbuf[c, k, i].astype(F32)

    pair.wait_send()
    pair2.wait_send()

    @pl.loop(1, R)
    def _(i):
        k = (chip + i) % R
        chip_copy(k).wait_send()
        back_copy(k).wait_send()

    @pl.loop(1, n)
    def _(i):
        cnt_copy((me + i) % n).wait_send()
    for m in range(2):
        for d in range(2):
            for u in range(subs):
                @pl.loop(0, R)
                def _(s):
                    sib_copy(m, d, s, u, core).wait_send()

                @pl.loop(0, R - 1)
                def _(s):
                    ring_copy(m, d, s, u).wait_send()


def per_device(n, tokens, targets, norm_gain, up_frozen, down_frozen,
               up_left, up_right, down_left, down_right, counts):
    R = n // 2
    tok, d = tokens.shape
    rank = up_left.shape[0]
    rows, ffl = up_frozen.shape
    cr = 2 * rows
    half = rows // 2
    subs = 2 if half % 32 == 0 else 1
    tile = 512 if ffl % 512 == 0 else 128
    n_blocks = 2 * (d + ffl) // 128
    bpd = -(-n_blocks // n)
    wide = tokens.astype(F32)
    scale = lax.rsqrt(jnp.mean(wide * wide, axis=1, keepdims=True) + NORM_EPS)
    nx = (wide * scale * norm_gain).astype(BF16)
    nx = nx.reshape(tok, R, cr).transpose(1, 0, 2)
    diff = (wide - targets.astype(F32)).reshape(tok, R, cr).transpose(1, 0, 2)
    cnt = jnp.broadcast_to(counts.astype(F32)[:, None], (8, 128))
    vm = pl.BlockSpec(memory_space=pltpu.VMEM)
    hbm = pl.BlockSpec(memory_space=pl.ANY)
    V = pltpu.VMEM
    dma = lambda *s: pltpu.SemaphoreType.DMA(s)
    return pl.pallas_call(
        functools.partial(kernel, n, subs, bpd, tile),
        out_shape=[jax.ShapeDtypeStruct(a.shape, F32)
                   for a in (up_left, up_right, down_left, down_right)],
        in_specs=[hbm, hbm] + [vm] * 7,
        out_specs=[vm] * 4,
        scratch_shapes=[
            V((R, cr, ffl), BF16), V((R, cr, ffl), BF16),
            V((tok, ffl), F32), V((tok, ffl), F32), V((tok, ffl), F32),
            V((tok, ffl), BF16),
            V((R, tok, cr), BF16), V((R, tok, cr), BF16), V((R, tok, cr), BF16),
            V((rank, d), F32), V((rank, ffl), F32), V((rank, ffl), F32), V((rank, d), F32),
            V((R, rank, cr), BF16), V((R, rank, cr), BF16), V((rank, ffl), BF16), V((rank, ffl), BF16),
            V((rank, tok), BF16), V((rank, tok), BF16), V((rank, tok), F32), V((tok, rank), BF16),
            V((2, rank, tok), F32), V((2, rank, tok), F32), V((n, 8, 128), F32),
            V((2, R, bpd, rank, 128), BF16), V((R, bpd, rank, 128), BF16),
            V((R, bpd, rank, 128), BF16), V((R, bpd, rank, 128), BF16),
            V((2, R, bpd, rank, 128), BF16),
            dma(2), dma(2, 2, R, subs), dma(2, 2, R, subs), dma(2, 2, R, subs), dma(2, 2, R, subs),
            dma(R), dma(R), dma(2), dma(2), dma(n), dma(n),
            dma(2), dma(2), dma(R), dma(R), dma(R), dma(R),
        ],
        compiler_params=pltpu.CompilerParams(
            vmem_limit_bytes=60 * 1024 * 1024, has_side_effects=True),
    )(up_frozen, down_frozen.T, nx, diff, up_left, up_right, down_left, down_right, cnt)


def solution(mesh):
    placed = (
        P("client", None),
        P("client", None),
        P(),
        P("client", "tp"),
        P("tp", "client"),
        P(),
        P(None, "tp"),
        P(None, "tp"),
        P(),
        P("client"),
    )
    return jax.shard_map(
        functools.partial(per_device, mesh.shape["client"]),
        mesh=mesh,
        in_specs=placed,
        out_specs=(P(), P(None, "tp"), P(None, "tp"), P()),
        check_vma=False,
    )
```

time: 625 us -> 284 us (0.45)
  waiting for transfers between devices: 401 us -> 0 us
  Pallas kernels: 0 us -> 265 us
  matrix products: 115 us -> 0 us
  blocking collectives: 81 us -> 0 us
  between operations: 15.6 us -> 1.32 us
  local copies, waits for them, and re-layouts: 6.61 us -> 14.4 us
    all_gather x5 -> x0, waiting for transfers between devices: 283 us -> none  [the longest x1 114 us: per_device(): whole_up = lax.all_gather(up_frozen, 'client', axis=0, tiled=True)]
    pallas_call x0 -> x1, Pallas kernels: none -> 265 us  [per_device(): pl.pallas_call(functools.partial(kernel, n, subs, bpd, tile), out_shape=[...]
    dot_general x40 -> x0, matrix products: 115 us -> none  [the longest x15 36.5 us: contract_columns(): lax.dot_general(left, right, (((1,), (1,)), ((), ())), preferred_element_...]
    psum x7 -> x0, blocking collectives: 81 us -> none  [the longest x1 32.8 us: per_device(): lax.psum((deltas[0], deltas[1], deltas[2], deltas[3], weight), 'client')]
    psum x1 -> x0, waiting for transfers between devices: 60 us -> none  [per_device(): lax.psum((deltas[0], deltas[1], deltas[2], deltas[3], weight), 'client')]
    reduce_scatter x3 -> x0, waiting for transfers between devices: 57.1 us -> none  [per_device(): lax.psum_scatter(partial_value, 'tp', scatter_dimension=1, tiled=True)]
  transfers between devices with their start and end apart: 9 -> 0, of which waited for: 9 -> 0; matrix products, arithmetic and copies ran while one was open for 4% -> 0% of each run, Pallas kernels for 0% -> 0%
where the time goes in v1:
time: 284 us; the launch traced here: 283 us
  Pallas kernels  265 us (93%)
  local copies, waits for them, and re-layouts  14.4 us (5%)
  other arithmetic  2.94 us (1%)
    pallas_call x1, Pallas kernels, per_device(): pl.pallas_call(functools.partial(kernel, n, subs, bpd, tile), out_shape=[...  265 us
    unnamed x15, local copies, waits for them, and re-layouts  10.6 us

profile of v1, /device:TPU:0, one launch (start us, length us, event | category | flops | bytes accessed | tf_op | source)
XLA Modules:
  0.0 283.3 jit_solution(7641477650256885909)
XLA Ops:
  0.6 0.0 copy-start.1
  0.6 1.6 copy.16
  2.2 0.0 copy-start.3
  2.2 0.3 fusion
  2.5 0.0 copy-done.1
  2.5 1.3 copy.18
  3.9 0.0 copy-done.3
  3.9 2.6 convert_subtract_fusion
  6.5 0.0 copy-start
  6.5 1.8 copy.19
  8.4 0.0 copy-start.2
  8.4 0.0 copy-done
  8.4 1.3 copy.17
  9.7 0.0 copy-done.2
  9.7 1.3 copy.15
  11.7 0.6 broadcast_in_dim.5.cnt
  12.2 264.6 %shard_map.129 = (f32[16,2048]{1,0:T(8,128)}, f32[16,3584]{1,0:T(8,128)}, f32[16,3584]{1,0:T(8,128)}, f32[16,2048]{1,0:T(8,128)}) custom-call(bf16[128,3584]{1,0:T(8,128)(2,1)} %up.1, bf16[128,3584]{1,0:T(8,128)(2,1)} %bitcast.10, bf16[8,256,256]{2,1,0:T(8,128)(2,1)} %bitcast.8, f32[8,256,256]{2,1,0:T(8,128)} %bitcast.6, f32[16,2048]{1,0:T(8,128)} %ul0.1, ...), custom_call_target="tpu_custom_call" | custom-call | tf_op jit(solution)/shard_map/pallas_call | solution.py:413
  276.9 1.6 copy.25
  278.5 1.6 copy.26
  280.1 1.6 copy.27
  281.7 1.6 copy.28
  (1 shorter events, 0.0 us)
Async XLA Ops:
  0.6 1.9 copy-start.1
  2.2 1.7 copy-start.3
  6.5 1.9 copy-start
  8.4 1.3 copy-start.2

commit v2 on v1

--- a/solution.py
+++ b/solution.py
@@ -36,7 +36,7 @@
            lut, ldt, dldt, ldm, xtx, xrx, cntb,
            sbuf, abuf, bbuf, cbuf, rbuf,
            own_s, ring_s, ring_r, sib_s, sib_r, p_s, p_r, x_s, x_r, c_s, c_r,
-           ab_s, ab_r, b_s, b_r, g_s, g_r):
+           ab_s, ab_r, b_s, b_r, g_s, g_r, o_s):
     R = n // 2
     half_ring = R // 2
     me = lax.axis_index("client")
@@ -92,8 +92,8 @@
             for d in range(2):
                 sib_copy(m, d, 0, u, core).start()
 
-    def advance(m, s, forward):
-        for u in range(subs):
+    def advance(m, s, forward, which=tuple(range(subs))):
+        for u in which:
             for d in range(2):
                 ring_arrived(m, d, s, u)
                 if forward:
@@ -217,25 +217,41 @@
         def _(j):
             copy(ptx.at[j], prx.at[j], p_s.at[j], p_r.at[j], me, 1 - tp).wait_send()
 
+    first, rest = (0,), tuple(range(1, subs))
+
     add_base(0)
 
     @pl.loop(1, half_ring)
     def _(s):
         advance(0, s, True)
     advance(0, half_ring, half_ring < R - 1)
-    add_base(half_ring)
 
     @pl.loop(half_ring + 1, R - 1)
     def _(s):
-        advance(0, s, True)
-        add_base(s)
-        add_base(R - s)
+        advance(0, s, True, first)
+
+        @pl.when(s == half_ring + 1)
+        def _():
+            add_base(half_ring)
+
+        @pl.when(s > half_ring + 1)
+        def _():
+            add_base(s - 1)
+        advance(0, s, True, rest)
+
+        @pl.when(s > half_ring + 1)
+        def _():
+            add_base(R - s + 1)
     own1.wait()
     send_own(1)
+    add_base(R - 2)
+    add_base(2)
     advance(0, R - 1, False)
     add_base(R - 1)
     add_base(1)
+    advance(1, 1, True, first)
     begin_step()
+    advance(1, 1, True, rest)
 
     def down_at(dist):
         return chip_at(pos - dist)
@@ -243,7 +259,6 @@
     sib_arrived(1, 0)
     forward_piece(chip)
 
-    advance(1, 1, True)
     take_low()
     backward_piece(chip)
 
@@ -256,27 +271,29 @@
 
     @pl.loop(half_ring + 1, R - 1)
     def _(s):
-        advance(1, s, True)
+        advance(1, s, True, first)
+
+        @pl.when(s == half_ring + 1)
+        def _():
+            backward_piece(down_at(half_ring))
+
+        @pl.when(s > half_ring + 1)
+        def _():
+            backward_piece(down_at(s - 1))
+            backward_piece(down_at(R - s + 1))
+        advance(1, s, True, rest)
         sib_arrived(1, s)
         forward_piece(down_at(s))
         sib_arrived(1, R - s)
         forward_piece(down_at(R - s))
-
-        @pl.when(s == half_ring + 1)
-        def _():
-            backward_piece(down_at(half_ring))
-
-        @pl.when(s > half_ring + 1)
-        def _():
-            backward_piece(down_at(s - 1))
-            backward_piece(down_at(R - s + 1))
-    advance(1, R - 1, False)
+    advance(1, R - 1, False, first)
+    backward_piece(down_at(R - 2))
+    backward_piece(down_at(2))
+    advance(1, R - 1, False, rest)
     sib_arrived(1, R - 1)
     forward_piece(down_at(R - 1))
     sib_arrived(1, 1)
     forward_piece(down_at(1))
-    backward_piece(down_at(R - 2))
-    backward_piece(down_at(2))
     backward_piece(down_at(R - 1))
     backward_piece(down_at(1))
     end_step()
@@ -361,8 +378,12 @@
     for b in range(len(blocks)):
         owner, i = divmod(b, bpd)
         c, k = divmod(owner, R)
-        _, _, result, cols = blocks[b]
-        result[:, cols] = rbuf[c, k, i].astype(F32)
+        value, _, _, cols = blocks[b]
+        value[:, cols] = rbuf[c, k, i].astype(F32)
+    outs = [pltpu.make_async_copy(v, o, o_s.at[i])
+            for i, (v, o) in enumerate(((ul, oul), (ur, our), (dl, odl), (dr, odr)))]
+    for o in outs:
+        o.start()
 
     pair.wait_send()
     pair2.wait_send()
@@ -386,6 +407,8 @@
                 @pl.loop(0, R - 1)
                 def _(s):
                     ring_copy(m, d, s, u).wait_send()
+    for o in outs:
+        o.wait()
 
 
 def per_device(n, tokens, targets, norm_gain, up_frozen, down_frozen,
@@ -415,7 +438,7 @@
         out_shape=[jax.ShapeDtypeStruct(a.shape, F32)
                    for a in (up_left, up_right, down_left, down_right)],
         in_specs=[hbm, hbm] + [vm] * 7,
-        out_specs=[vm] * 4,
+        out_specs=[pl.BlockSpec(memory_space=pltpu.HBM)] * 4,
         scratch_shapes=[
             V((R, cr, ffl), BF16), V((R, cr, ffl), BF16),
             V((tok, ffl), F32), V((tok, ffl), F32), V((tok, ffl), F32),
@@ -430,7 +453,7 @@
             V((2, R, bpd, rank, 128), BF16),
             dma(2), dma(2, 2, R, subs), dma(2, 2, R, subs), dma(2, 2, R, subs), dma(2, 2, R, subs),
             dma(R), dma(R), dma(2), dma(2), dma(n), dma(n),
-            dma(2), dma(2), dma(R), dma(R), dma(R), dma(R),
+            dma(2), dma(2), dma(R), dma(R), dma(R), dma(R), dma(4),
         ],
         compiler_params=pltpu.CompilerParams(
             vmem_limit_bytes=60 * 1024 * 1024, has_side_effects=True),

time: 284 us -> 286 us (level)
  no operation moved by 1% of the time
where the time goes in v2:
time: 286 us
  Pallas kernels  267 us (93%)
  local copies, waits for them, and re-layouts  14.4 us (5%)
  other arithmetic  2.94 us (1%)
    pallas_call x1, Pallas kernels, per_device(): pl.pallas_call(functools.partial(kernel, n, subs, bpd, tile), out_shape=[...  267 us
    unnamed x15, local copies, waits for them, and re-layouts  10.6 us

profile of v2, /device:TPU:0, one launch (start us, length us, event | category | flops | bytes accessed | tf_op | source)
XLA Modules:
  0.0 285.7 jit_solution(17433331779283659419)
XLA Ops:
  0.6 0.0 copy-start.1
  0.6 1.6 copy.16
  2.2 0.0 copy-start.3
  2.2 0.3 fusion
  2.5 0.0 copy-done.1
  2.5 1.3 copy.18
  3.9 0.0 copy-done.3
  3.9 2.6 convert_subtract_fusion
  6.5 0.0 copy-start
  6.5 1.8 copy.19
  8.4 0.0 copy-start.2
  8.4 0.0 copy-done
  8.4 1.3 copy.17
  9.7 0.0 copy-done.2
  9.7 1.3 copy.15
  11.7 0.6 broadcast_in_dim.5.cnt
  12.2 267.0 %shard_map.129 = (f32[16,2048]{1,0:T(8,128)}, f32[16,3584]{1,0:T(8,128)}, f32[16,3584]{1,0:T(8,128)}, f32[16,2048]{1,0:T(8,128)}) custom-call(bf16[128,3584]{1,0:T(8,128)(2,1)} %up.1, bf16[128,3584]{1,0:T(8,128)(2,1)} %bitcast.10, bf16[8,256,256]{2,1,0:T(8,128)(2,1)} %bitcast.8, f32[8,256,256]{2,1,0:T(8,128)} %bitcast.6, f32[16,2048]{1,0:T(8,128)} %ul0.1, ...), custom_call_target="tpu_custom_call" | custom-call | tf_op jit(solution)/shard_map/pallas_call | solution.py:436
  279.2 1.6 copy.25
  280.8 1.6 copy.26
  282.5 1.6 copy.27
  284.1 1.6 copy.28
  (1 shorter events, 0.0 us)
Async XLA Ops:
  0.6 1.9 copy-start.1
  2.2 1.7 copy-start.3
  6.5 1.9 copy-start
  8.4 1.3 copy-start.2
